TPU v7x, 32 devices: a whole 2x2x4 slice. The times are simulated.
32 devices in a mesh: lon: 16 (over z, y, core), lat: 2 (over x).
Axes of the slice: x: 2, y: 2, z: 4, core: 2. Of those that a mesh axis runs over, the one named last changes fastest.
Arguments:
- fields: bfloat16 [256, 512, 256], P('lat', 'lon'), may hold values from -6 to 6
- spec_weight: bfloat16 [2, 2, 17, 256, 256], replicated, may hold values from -0.75 to 0.75
- skip_weight: bfloat16 [2, 256, 256], replicated, may hold values from -0.375 to 0.375
- diffusion: float32 [2, 256], replicated, may hold values from 0.2 to 1
Outputs:
- result: bfloat16 [256, 512, 256], P('lat', 'lon')
All inputs are finite; a program needn't handle non-finite values.
Results may differ from a plain program's by a relative error of at most 0.01.
Values may be sent and summed in bfloat16 or wider, within the bound.
A program may use at most 128 MiB of HBM per device.

v0:
```python
import functools

import jax
import jax.numpy as jnp
import ml_dtypes
import numpy as np
from jax import lax
from jax.experimental import pallas as pl
from jax.experimental.pallas import tpu as pltpu
from jax.sharding import PartitionSpec as P

WINDOW = 64
HOP = 32
MODES = 17
LAYERS = 2
GROUP = 4
STRIPS = 2 * GROUP
COEFS = 2 * MODES
CHUNKS = 4

def tables():
    points = np.arange(WINDOW, dtype=np.float64)
    freqs = np.arange(MODES, dtype=np.float64)
    angles = 2.0 * np.pi * points[:, None] * freqs[None, :] / WINDOW
    taper = 0.5 - 0.5 * np.cos(2.0 * np.pi * points / WINDOW)
    analysis = np.concatenate(
        [taper[:, None] * np.cos(angles), -taper[:, None] * np.sin(angles)], axis=1
    )
    factor = np.where(freqs == 0.0, 1.0, 2.0) / WINDOW
    synthesis = np.concatenate(
        [factor[:, None] * np.cos(angles).T, -factor[:, None] * np.sin(angles).T], axis=0
    )
    return analysis, synthesis


def banded_tables():
    analysis, synthesis = tables()
    length = STRIPS * HOP
    forward = np.zeros((COEFS, STRIPS, length))
    backward = np.zeros((length, COEFS, STRIPS))
    for f in range(STRIPS):
        cells = (f * HOP + np.arange(WINDOW)) % length
        forward[:, f, cells] = analysis.T
        backward[cells, :, f] = synthesis.T
    kind = ml_dtypes.bfloat16
    forward = forward.reshape(COEFS * STRIPS, length).astype(np.float32).astype(kind)
    backward = backward.reshape(length, COEFS * STRIPS).astype(np.float32).astype(kind)
    return forward, backward


def gelu(x):
    return jax.nn.gelu(x, approximate=True)


def layer_rows(rows, first, source, source_lo, target, target_first, lo, hi, forward, backward, spec, skip, diff, coefs, valid):
    channels = skip.shape[-1]
    pairs = rows // 2

    def analyse(pair, carry):
        parts = []
        for half in range(2):
            x = source[first + 2 * pair + half + 1]
            part = jnp.dot(forward[...], x, preferred_element_type=jnp.float32)
            parts.append(part.reshape(COEFS, STRIPS, channels))
        both = jnp.concatenate(parts, axis=1).astype(jnp.bfloat16)
        coefs[:, pl.ds(pl.multiple_of(pair * 2 * STRIPS, 2 * STRIPS), 2 * STRIPS), :] = both
        return carry

    lax.fori_loop(0, pairs, analyse, 0)

    used = rows * STRIPS

    def mix(k, carry):
        real = coefs[k, :used]
        imag = coefs[MODES + k, :used]
        weight_real = spec[0, k]
        weight_imag = spec[1, k]
        dot = functools.partial(jnp.dot, preferred_element_type=jnp.float32)
        mixed_real = dot(real, weight_real) - dot(imag, weight_imag)
        mixed_imag = dot(real, weight_imag) + dot(imag, weight_real)
        coefs[k, :used] = mixed_real.astype(jnp.bfloat16)
        coefs[MODES + k, :used] = mixed_imag.astype(jnp.bfloat16)
        return carry

    lax.fori_loop(0, MODES, mix, 0)

    def synthesise(pair, carry):
        both = coefs[:, pl.ds(pl.multiple_of(pair * 2 * STRIPS, 2 * STRIPS), 2 * STRIPS), :].astype(jnp.float32)
        for half in range(2):
            row = 2 * pair + half
            mixed = both[:, half * STRIPS : (half + 1) * STRIPS]
            mixed = mixed.reshape(COEFS * STRIPS, channels).astype(jnp.bfloat16)
            cells = pl.ds(lo - source_lo, hi - lo)
            centre = source[first + row + 1, cells]
            hidden = jnp.dot(backward[lo:hi], mixed, preferred_element_type=jnp.float32)
            hidden = hidden + jnp.dot(centre, skip[...], preferred_element_type=jnp.float32)
            wide = centre.astype(jnp.float32)
            laplacian = (
                source[first + row + 2, cells].astype(jnp.float32) + source[first + row, cells].astype(jnp.float32) - 2.0 * wide
            )
            hidden = hidden + diff * laplacian
            result = wide + gelu(hidden)
            if valid is not None:
                result = jnp.where(valid(row), result, 0.0)
            target[target_first + row] = result.astype(jnp.bfloat16)
        return carry

    lax.fori_loop(0, pairs, synthesise, 0)


def kernel(
    group_rows, band_rows, grid_rows, count, lats,
    padded, spec_hbm, skip, diffusion, forward, forward_inner, backward,
    result,
    window, middle, final, coefs, spec, edges,
    spec_sems, own_sems, put_sems, y_send, y_recv, z_send, z_recv, lat_send, lat_recv, out_send, out_recv,
):
    index = lax.axis_index("lon")
    lat = lax.axis_index("lat")
    place = lax.rem(index, GROUP)
    base = index - place
    quarter = group_rows // CHUNKS
    length = STRIPS * HOP
    pieces = [
        (quarter, quarter + 4),
        (2 * quarter + 4, quarter),
        (0, quarter),
        (3 * quarter + 4, quarter),
    ]
    upward = lax.rem(index + GROUP, count)
    downward = lax.rem(index + count - GROUP, count)

    def xor(d):
        low = lax.rem(place, 2)
        high = place // 2
        low = 1 - low if d & 1 else low
        high = 1 - high if d & 2 else high
        return 2 * high + low

    def strip(at):
        return pl.ds(pl.multiple_of((at + 2) * HOP, HOP), HOP)

    def remote(source, target, send, recv, where):
        return pltpu.make_async_remote_copy(
            src_ref=source, dst_ref=target, send_sem=send, recv_sem=recv,
            device_id=where, device_id_type=pl.DeviceIdType.MESH,
        )

    def y_copy(n, d, receive):
        first, number = pieces[n]
        other = xor(d)
        owner = other if receive else place
        return remote(
            padded.at[pl.ds(other * group_rows + first, number)],
            window.at[pl.ds(first, number), strip(owner)],
            y_send.at[n, d], y_recv.at[n, d], {"lon": base + other},
        )

    def z_copy(n, side, receive):
        first, number = pieces[n]
        rows = pl.ds(first, number)
        if side == 0:
            source, target, where = 4 * HOP, 0, upward
        else:
            source, target, where = 2 * HOP, 6 * HOP, downward
        return remote(
            window.at[rows, pl.ds(source, 2 * HOP)],
            window.at[rows, pl.ds(target, 2 * HOP)],
            z_send.at[n, side], z_recv.at[n, side], {"lon": where},
        )

    def out_copy(chunk, d, receive):
        other = xor(d)
        owner = other if receive else place
        return remote(
            final.at[pl.ds(chunk * quarter, quarter), pl.ds(pl.multiple_of(other * HOP, HOP), HOP)],
            result.at[pl.ds(owner * group_rows + chunk * quarter, quarter)],
            out_send.at[chunk, d], out_recv.at[chunk, d], {"lon": base + other},
        )

    own = []
    for n in range(CHUNKS):
        first, number = pieces[n]
        for d in (2, 3, 1):
            y_copy(n, d, False).start()
        copy = pltpu.make_async_copy(
            padded.at[pl.ds(place * group_rows + first, number)],
            window.at[pl.ds(first, number), strip(place)],
            own_sems.at[n],
        )
        copy.start()
        own.append(copy)
    loads = []
    for layer in range(LAYERS):
        copy = pltpu.make_async_copy(spec_hbm.at[layer], spec.at[layer], spec_sems.at[layer])
        copy.start()
        loads.append(copy)

    for n in range(CHUNKS):
        own[n].wait()
        for d in (1, 2, 3):
            y_copy(n, d, True).wait_recv()
        for side in range(2):
            z_copy(n, side, False).start()

    low_edge = jnp.logical_and(place == 0, lat > 0)
    high_edge = jnp.logical_and(place == GROUP - 1, lat < lats - 1)

    def to_before():
        return remote(
            window.at[pl.ds(2, 2)], edges.at[1], lat_send.at[0], lat_recv.at[1],
            {"lon": base + GROUP - 1, "lat": jnp.maximum(lat - 1, 0)},
        )

    def to_after():
        return remote(
            window.at[pl.ds(group_rows, 2)], edges.at[0], lat_send.at[1], lat_recv.at[0],
            {"lon": base, "lat": jnp.minimum(lat + 1, lats - 1)},
        )

    def run(chunk):
        start = chunk * quarter
        top = lat * band_rows + place * group_rows + start - 1

        def valid(row):
            at = top + row
            return jnp.logical_and(at >= 0, at < grid_rows)

        layer_rows(
            quarter + 2, start, window, 0, middle, 0, HOP, length - HOP, forward, backward,
            spec.at[0], skip.at[0], diffusion[0:1], coefs, valid,
        )
        layer_rows(
            quarter, 0, middle, HOP, final, start, 2 * HOP, length - 2 * HOP, forward_inner, backward,
            spec.at[1], skip.at[1], diffusion[1:2], coefs, None,
        )
        for d in (2, 3, 1):
            out_copy(chunk, d, False).start()
        put = pltpu.make_async_copy(
            final.at[pl.ds(start, quarter), pl.ds(pl.multiple_of(place * HOP, HOP), HOP)],
            result.at[pl.ds(place * group_rows + start, quarter)],
            put_sems.at[chunk],
        )
        put.start()
        return put

    def arrived(n):
        for side in range(2):
            z_copy(n, side, True).wait_recv()
            z_copy(n, side, False).wait_send()

    puts = []
    arrived(0)
    for copy in loads:
        copy.wait()
    puts.append(run(1))
    arrived(1)
    puts.append(run(2))
    arrived(2)

    @pl.when(low_edge)
    def _():
        to_before().start()

    arrived(3)

    @pl.when(high_edge)
    def _():
        to_after().start()
        to_before().wait_recv()
        window[group_rows + 2 : group_rows + 4] = edges[1]

    puts.append(run(3))

    @pl.when(low_edge)
    def _():
        to_after().wait_recv()
        window[0:2] = edges[0]

    puts.append(run(0))

    for put in puts:
        put.wait()

    @pl.when(low_edge)
    def _():
        to_before().wait_send()

    @pl.when(high_edge)
    def _():
        to_after().wait_send()

    for n in range(CHUNKS):
        for d in (1, 2, 3):
            y_copy(n, d, False).wait_send()
            out_copy(n, d, False).wait_send()
    for n in range(CHUNKS):
        for d in (1, 2, 3):
            out_copy(n, d, True).wait_recv()


def local(grid_rows, fields, spec_weight, skip_weight, diffusion):
    band_rows, strip, channels = fields.shape
    group_rows = band_rows // GROUP
    quarter = group_rows // CHUNKS
    length = STRIPS * HOP
    forward, backward = banded_tables()
    consts = (jnp.asarray(forward), jnp.asarray(forward[:, HOP:-HOP]), jnp.asarray(backward))
    padded = jnp.pad(fields, ((2, 2), (0, 0), (0, 0)))
    anywhere = pl.BlockSpec(memory_space=pl.ANY)
    inside = pl.BlockSpec(memory_space=pltpu.VMEM)
    dma = pltpu.SemaphoreType.DMA
    return pl.pallas_call(
        functools.partial(
            kernel, group_rows, band_rows, grid_rows, lax.axis_size("lon"), lax.axis_size("lat")
        ),
        out_shape=jax.ShapeDtypeStruct(fields.shape, jnp.bfloat16),
        in_specs=[anywhere] * 2 + [inside] * 5,
        out_specs=anywhere,
        scratch_shapes=[
            pltpu.VMEM((group_rows + 4, length, channels), jnp.bfloat16),
            pltpu.VMEM((quarter + 2, length - 2 * HOP, channels), jnp.bfloat16),
            pltpu.VMEM((group_rows, length - 4 * HOP, channels), jnp.bfloat16),
            pltpu.VMEM((COEFS, (quarter + 2) * STRIPS, channels), jnp.bfloat16),
            pltpu.VMEM(spec_weight.shape, jnp.bfloat16),
            pltpu.VMEM((2, 2, length, channels), jnp.bfloat16),
            dma((LAYERS,)), dma((CHUNKS,)), dma((CHUNKS,)),
            dma((CHUNKS, GROUP)), dma((CHUNKS, GROUP)),
            dma((CHUNKS, 2)), dma((CHUNKS, 2)),
            dma((2,)), dma((2,)),
            dma((CHUNKS, GROUP)), dma((CHUNKS, GROUP)),
        ],
        compiler_params=pltpu.CompilerParams(
            vmem_limit_bytes=56 * 1024 * 1024, has_side_effects=True
        ),
    )(padded, spec_weight, skip_weight, diffusion, *consts)


def solution(mesh):
    in_specs = (P("lat", "lon", None), P(), P(), P())
    out_specs = P("lat", "lon", None)

    def whole(fields, spec_weight, skip_weight, diffusion):
        step = functools.partial(local, fields.shape[0])
        return jax.shard_map(step, mesh=mesh, in_specs=in_specs, out_specs=out_specs, check_vma=False)(
            fields, spec_weight, skip_weight, diffusion
        )

    return whole
```

profile of v0, /device:TPU:0, one launch (start us, length us, event | category | flops | bytes accessed | tf_op | source)
XLA Modules:
  0.0 113.5 jit_solution(2703275912030827093)
XLA Ops:
  0.0 3.1 %pad.4.padded = bf16[132,32,256]{2,1,0:T(8,128)(2,1)} pad(bf16[128,32,256]{2,1,0:T(8,128)(2,1)} %param.7, bf16[]{:T(256)} %constant.8.clone.1), padding=2_2x0_0x0_0 | pad | bytes 4259842 | tf_op jit(solution)/shard_map/jit(_pad)/pad | solution.py:309
  3.1 107.3 %shard_map.73 = bf16[128,32,256]{2,1,0:T(8,128)(2,1)} custom-call(bf16[132,32,256]{2,1,0:T(8,128)(2,1)} %pad.4.padded, bf16[2,2,17,256,256]{4,3,2,1,0:T(8,128)(2,1)} %spec_hbm.1, bf16[2,256,256]{2,1,0:T(8,128)(2,1)} %skip.1, f32[2,256]{1,0:T(2,128)} %diffusion.1, bf16[272,256]{1,0:T(8,128)(2,1)} %constant.9.clone.forward, ...), custom_call_target="tpu_custom_call" | custom-call | tf_op jit(solution)/shard_map/pallas_call | solution.py:313
  110.4 3.1 %copy.9 = bf16[128,32,256]{2,1,0:T(8,128)(2,1)} copy(bf16[128,32,256]{2,1,0:T(8,128)(2,1)} %shard_map.73) | data formatting | bytes 4194304
where the time goes:
time: 114 us; the launch traced here: 113 us
  Pallas kernels  107 us (94%)
  local copies, waits for them, and re-layouts  6.2 us (5%)
    pallas_call x1, Pallas kernels, local(): pl.pallas_call(functools.partial(kernel, group_rows, band_rows, grid_rows...  107 us
    pad x1, local copies, waits for them, and re-layouts, local(): padded = jnp.pad(fields, ((2, 2), (0, 0), (0, 0)))  3.12 us
    unnamed x1, local copies, waits for them, and re-layouts  3.08 us

commit v1 on v0

--- a/solution.py
+++ b/solution.py
@@ -17,6 +17,7 @@
 STRIPS = 2 * GROUP
 COEFS = 2 * MODES
 CHUNKS = 4
+UNROLL = 17
 
 def tables():
     points = np.arange(WINDOW, dtype=np.float64)
@@ -63,29 +64,36 @@
             part = jnp.dot(forward[...], x, preferred_element_type=jnp.float32)
             parts.append(part.reshape(COEFS, STRIPS, channels))
         both = jnp.concatenate(parts, axis=1).astype(jnp.bfloat16)
-        coefs[:, pl.ds(pl.multiple_of(pair * 2 * STRIPS, 2 * STRIPS), 2 * STRIPS), :] = both
+        coefs[:, pl.ds(pair * 2 * STRIPS, 2 * STRIPS), :] = both
         return carry
 
-    lax.fori_loop(0, pairs, analyse, 0)
+    for pair in range(pairs):
+        analyse(pair, None)
 
     used = rows * STRIPS
 
     def mix(k, carry):
         real = coefs[k, :used]
         imag = coefs[MODES + k, :used]
-        weight_real = spec[0, k]
-        weight_imag = spec[1, k]
-        dot = functools.partial(jnp.dot, preferred_element_type=jnp.float32)
-        mixed_real = dot(real, weight_real) - dot(imag, weight_imag)
-        mixed_imag = dot(real, weight_imag) + dot(imag, weight_real)
-        coefs[k, :used] = mixed_real.astype(jnp.bfloat16)
-        coefs[MODES + k, :used] = mixed_imag.astype(jnp.bfloat16)
+        weights = jnp.concatenate([spec[0, k], spec[1, k]], axis=0)
+        both = jnp.concatenate(
+            [jnp.concatenate([real, -imag], axis=1), jnp.concatenate([imag, real], axis=1)], axis=0
+        )
+        mixed = jnp.dot(both, weights, preferred_element_type=jnp.float32).astype(jnp.bfloat16)
+        coefs[k, :used] = mixed[:used]
+        coefs[MODES + k, :used] = mixed[used:]
+
+    def mix_some(step, carry):
+        for k in range(UNROLL):
+            mix(step * UNROLL + k, None)
         return carry
 
-    lax.fori_loop(0, MODES, mix, 0)
+    lax.fori_loop(0, MODES // UNROLL, mix_some, 0)
+    for k in range(MODES // UNROLL * UNROLL, MODES):
+        mix(k, None)
 
     def synthesise(pair, carry):
-        both = coefs[:, pl.ds(pl.multiple_of(pair * 2 * STRIPS, 2 * STRIPS), 2 * STRIPS), :].astype(jnp.float32)
+        both = coefs[:, pl.ds(pair * 2 * STRIPS, 2 * STRIPS), :].astype(jnp.float32)
         for half in range(2):
             row = 2 * pair + half
             mixed = both[:, half * STRIPS : (half + 1) * STRIPS]
@@ -105,7 +113,8 @@
             target[target_first + row] = result.astype(jnp.bfloat16)
         return carry
 
-    lax.fori_loop(0, pairs, synthesise, 0)
+    for pair in range(pairs):
+        synthesise(pair, None)
 
 
 def kernel(
@@ -196,13 +205,16 @@
         copy.start()
         loads.append(copy)
 
-    for n in range(CHUNKS):
+    def forward_piece(n):
         own[n].wait()
         for d in (1, 2, 3):
             y_copy(n, d, True).wait_recv()
         for side in range(2):
             z_copy(n, side, False).start()
 
+    forward_piece(0)
+    forward_piece(1)
+
     low_edge = jnp.logical_and(place == 0, lat > 0)
     high_edge = jnp.logical_and(place == GROUP - 1, lat < lats - 1)
 
@@ -218,7 +230,7 @@
             {"lon": base, "lat": jnp.minimum(lat + 1, lats - 1)},
         )
 
-    def run(chunk):
+    def run(chunk, between=None):
         start = chunk * quarter
         top = lat * band_rows + place * group_rows + start - 1
 
@@ -230,6 +242,8 @@
             quarter + 2, start, window, 0, middle, 0, HOP, length - HOP, forward, backward,
             spec.at[0], skip.at[0], diffusion[0:1], coefs, valid,
         )
+        if between is not None:
+            between()
         layer_rows(
             quarter, 0, middle, HOP, final, start, 2 * HOP, length - 2 * HOP, forward_inner, backward,
             spec.at[1], skip.at[1], diffusion[1:2], coefs, None,
@@ -253,7 +267,8 @@
     arrived(0)
     for copy in loads:
         copy.wait()
-    puts.append(run(1))
+    puts.append(run(1, lambda: forward_piece(2)))
+    forward_piece(3)
     arrived(1)
     puts.append(run(2))
     arrived(2)

time: 114 us -> 96.8 us (0.85)
  Pallas kernels: 107 us -> 90.4 us
    pallas_call x1, Pallas kernels: 107 us -> 90.4 us  [local(): pl.pallas_call(functools.partial(kernel, group_rows, band_rows, grid_rows...]
where the time goes in v1:
time: 96.8 us; the launch traced here: 96.7 us
  Pallas kernels  90.4 us (93%)
  local copies, waits for them, and re-layouts  6.2 us (6%)
    pallas_call x1, Pallas kernels, local(): pl.pallas_call(functools.partial(kernel, group_rows, band_rows, grid_rows...  90.4 us
    pad x1, local copies, waits for them, and re-layouts, local(): padded = jnp.pad(fields, ((2, 2), (0, 0), (0, 0)))  3.12 us
    unnamed x1, local copies, waits for them, and re-layouts  3.08 us

profile of v1, /device:TPU:0, one launch (start us, length us, event | category | flops | bytes accessed | tf_op | source)
XLA Modules:
  0.0 96.7 jit_solution(3096170015384816254)
XLA Ops:
  0.0 3.1 %pad.4.padded = bf16[132,32,256]{2,1,0:T(8,128)(2,1)} pad(bf16[128,32,256]{2,1,0:T(8,128)(2,1)} %param.7, bf16[]{:T(256)} %constant.8.clone.1), padding=2_2x0_0x0_0 | pad | bytes 4259842 | tf_op jit(solution)/shard_map/jit(_pad)/pad | solution.py:324
  3.1 90.4 %shard_map.73 = bf16[128,32,256]{2,1,0:T(8,128)(2,1)} custom-call(bf16[132,32,256]{2,1,0:T(8,128)(2,1)} %pad.4.padded, bf16[2,2,17,256,256]{4,3,2,1,0:T(8,128)(2,1)} %spec_hbm.1, bf16[2,256,256]{2,1,0:T(8,128)(2,1)} %skip.1, f32[2,256]{1,0:T(2,128)} %diffusion.1, bf16[272,256]{1,0:T(8,128)(2,1)} %constant.9.clone.forward, ...), custom_call_target="tpu_custom_call" | custom-call | tf_op jit(solution)/shard_map/pallas_call | solution.py:328
  93.6 3.1 %copy.9 = bf16[128,32,256]{2,1,0:T(8,128)(2,1)} copy(bf16[128,32,256]{2,1,0:T(8,128)(2,1)} %shard_map.73) | data formatting | bytes 4194304
